TPU v7x, 32 devices: a whole 2x2x4 slice. The times are simulated.
32 devices in a mesh: tok: 16 (over z, x, core), blk: 2 (over y).
Axes of the slice: x: 2, y: 2, z: 4, core: 2. Of those that a mesh axis runs over, the one named last changes fastest.
Arguments:
- activations: bfloat16 [2048, 7168], P('tok', 'blk'), may hold values from -600 to 600
- signs: float32 [7168], P('blk'), may hold values from -1 to 1, as said below
Outputs:
- hessian: float32 [7168, 7168], P('tok', 'blk')
- incoherence: float32 [7168], P('blk')
- largest_ratio: float32 [], replicated
Inputs may be any that keep to these rules, and one draw needn't show every extreme that they name: `signs`: every entry is -1 or 1.
All inputs are finite; a program needn't handle non-finite values.
Results may differ from a plain program's by a relative error of at most 0.0037.
Values may be sent and summed in bfloat16 or wider, within the bound.
A program may use at most 640 MiB of HBM per device.

v0:
```python
import math

import jax
import jax.numpy as jnp
from jax import lax
from jax.sharding import PartitionSpec as P

WALSH = 512
MIX = 14
FEATURES = 7168


EPS = 1e-06
DAMP = 0.01


def swapped(block, axis, distance):
    count = lax.axis_size(axis)
    route = []
    for low in range(count):
        high = low | 1 << distance
        if high != low and high < count:
            route += [(low, high), (high, low)]
    return lax.ppermute(block, axis, route)


def from_root(value, axis, source):
    kept = jnp.where(lax.axis_index(axis) == source, value, 0).astype(value.dtype)
    return lax.psum(kept, axis)


def walsh_table(length):
    position = jnp.arange(length, dtype=jnp.int32)
    parity = jnp.zeros((length, length), jnp.int32)
    for bit_number in range(length.bit_length() - 1):
        parity = parity + (position[:, None] >> bit_number & 1) * (
            position[None, :] >> bit_number & 1
        )
    return (1 - 2 * (parity % 2)).astype(jnp.float32)


def cosine_table(length):
    rows_idx = jnp.arange(length, dtype=jnp.float32)[:, None]
    columns = jnp.arange(length, dtype=jnp.float32)[None, :]
    table = math.sqrt(2.0 / length) * jnp.cos(math.pi * (columns + 0.5) * rows_idx / length)
    return jnp.where(rows_idx == 0.0, table * math.sqrt(0.5), table)


def contract_tokens(left, right):
    return lax.dot_general(
        left, right, (((0,), (0,)), ((), ())), preferred_element_type=jnp.float32
    )


def per_device(activations, signs):
    tok_rows, block_width = activations.shape
    blocks = lax.axis_size("blk")
    block_index = lax.axis_index("blk")
    token_groups = lax.axis_size("tok")
    token_index = lax.axis_index("tok")
    local_walsh = WALSH // blocks
    signed = activations * signs.astype(jnp.bfloat16)[None, :]
    local_table = jnp.kron(walsh_table(local_walsh) / math.sqrt(local_walsh), cosine_table(MIX).T)
    partial_mix = jnp.dot(signed.astype(jnp.float32), local_table, precision=lax.Precision.HIGHEST)
    for bit_number in range(blocks.bit_length() - 1):
        partner = swapped(partial_mix, "blk", bit_number)
        upper = block_index >> bit_number & 1 == 1
        partial_mix = jnp.where(upper, partner - partial_mix, partial_mix + partner)
    rotated = (partial_mix / math.sqrt(blocks)).astype(jnp.bfloat16)
    row_count = FEATURES // token_groups
    all_tokens = lax.all_gather(rotated, "tok", axis=0, tiled=True)
    first_row = token_index * row_count
    owner = first_row // block_width
    offset = first_row - owner * block_width
    own_slice = lax.dynamic_slice_in_dim(all_tokens, offset, row_count, 1)
    row_slice = from_root(own_slice, "blk", owner)
    gram_block = contract_tokens(row_slice, all_tokens)
    global_rows = token_index * row_count + jnp.arange(row_count, dtype=jnp.int32)[:, None]
    global_columns = block_index * block_width + jnp.arange(block_width, dtype=jnp.int32)[None, :]
    on_diag = global_rows == global_columns
    local_peaks = jnp.max(jnp.where(on_diag, 0.0, jnp.abs(gram_block)), axis=0)
    column_peak = lax.pmax(local_peaks, "tok")
    trace_total = lax.psum(jnp.sum(jnp.where(on_diag, gram_block, 0.0)), ("tok", "blk"))
    diag_mean = trace_total / FEATURES + EPS
    hessian = gram_block / diag_mean + DAMP * on_diag.astype(jnp.float32)
    incoherence = column_peak / diag_mean
    largest_ratio = lax.pmax(jnp.max(incoherence), "blk")
    return (hessian, incoherence, largest_ratio)


def solution(mesh):
    in_specs = (P("tok", "blk"), P("blk"))
    out_specs = (P("tok", "blk"), P("blk"), P())
    return jax.shard_map(
        per_device, mesh=mesh, in_specs=in_specs, out_specs=out_specs, check_vma=False
    )
```

profile of v0, /device:TPU:12, one launch (start us, length us, event | category | flops | bytes accessed | tf_op | source)
XLA Modules:
  0.0 860.5 jit_solution(9639242708453909916)
XLA Ops:
  7.2 0.0 all-gather.2.cloned.1.call-start
  7.3 0.1 multiply_select_fusion
  7.4 0.4 fusion.10
  7.8 142.1 %broadcast_multiply_fusion = f32[256,14,256,14]{3,2,1,0:T(8,128)} fusion(f32[14,14]{1,0:T(8,128)S(1)} %multiply_select_fusion, f32[256,256]{1,0:T(8,128)S(1)} %fusion.10), kind=kLoop, calls=%fused_computation | loop fusion | flops 12845056 | bytes 51643152 | tf_op jit(solution)/shard_map/jit(kron)/mul | solution.py:63
  149.9 0.0 copy-start.1
  149.9 0.0 copy-start
  149.9 326.1 %mul.279 = f32[3584,3584]{1,0:T(8,128)} reshape(f32[256,14,256,14]{3,2,1,0:T(8,128)} %broadcast_multiply_fusion) | data formatting | bytes 102760448 | tf_op jit(solution)/shard_map/jit(kron)/mul | solution.py:63
  476.0 0.0 copy-done.1
  476.0 0.0 copy-done
  476.0 24.3 %fusion.3 = f32[128,3584]{1,0:T(8,128)S(1)} fusion(f32[3584,3584]{1,0:T(8,128)} %mul.279, bf16[128,3584]{1,0:T(8,128)(2,1)S(1)} %copy-done, bf16[3584]{0:T(1024)(128)(2,1)S(1)} %convert_element_type.17), kind=kOutput, calls=%fused_computation.9 | convolution fusion | flops 19730464768 | bytes 54139904 | tf_op jit(solution)/shard_map/dot_general | solution.py:64
  500.3 0.6 collective-permute-start
  500.9 41.4 %collective-permute-done = f32[128,3584]{1,0:T(8,128)} collective-permute-done((f32[128,3584]{1,0:T(8,128)S(1)}, f32[128,3584]{1,0:T(8,128)}, u32[]{:S(2)}, u32[]{:S(2)}) %collective-permute-start) | collective-permute-done | bytes 1835040 | tf_op jit(solution)/shard_map/ppermute | solution.py:24
  542.2 2.7 multiply_convert_fusion
  544.9 0.0 all-gather.2.cloned.1.call-update
  545.0 0.2 all-reduce.2.cloned.1.call-start
  545.2 112.9 %all-gather.2.cloned.1.call-done = bf16[2048,3584]{1,0:T(8,128)(2,1)} async-done(((bf16[128,3584]{1,0:T(8,128)(2,1)}), bf16[2048,3584]{1,0:T(8,128)(2,1)}) %all-gather.2.cloned.1.call-update) | async-done | bytes 14680080 | tf_op jit(solution)/shard_map/all_gather | solution.py:71
  658.2 4.4 dynamic-slice_select_fusion
  662.6 0.0 all-reduce.2.cloned.1.call-update
  662.6 61.7 %all-reduce.2.cloned.1.call-done = bf16[2048,448]{1,0:T(8,128)(2,1)} async-done(((bf16[2048,448]{1,0:T(8,128)(2,1)}), bf16[2048,448]{1,0:T(8,128)(2,1)}) %all-reduce.2.cloned.1.call-update) | async-done | bytes 1835024 | tf_op jit(solution)/shard_map/psum | solution.py:29
  724.4 14.1 %fusion.2 = (f32[3584]{0:T(1024)S(1)}, f32[]{:T(128)}, f32[448,3584]{1,0:T(8,128)}) fusion(s32[3584]{0:T(1024)S(1)} %iota_add_fusion, s32[448]{0:T(512)S(1)} %iota_add_fusion.1, bf16[2048,448]{1,0:T(8,128)(2,1)} %all-reduce.2.cloned.1.call-done, bf16[2048,3584]{1,0:T(8,128)(2,1)} %all-gather.2.cloned.1.call-done), kind=kOutput, calls=%fused_computation.6 | convolution fusion | flops 6586298880 | bytes 22968068 | tf_op jit(solution)/shard_map/dot_general | solution.py:50
  738.4 53.1 %pmax.14 = f32[3584]{0:T(1024)S(1)} all-reduce(f32[3584]{0:T(1024)S(1)} %get-tuple-element.3), channel_id=1, replica_groups=mesh['tok'=16,'blk'=2] {'tok'}, use_global_device_ids=true, to_apply=%region_4.5 | all-reduce | flops 3584 | bytes 28672 | tf_op jit(solution)/shard_map/pmax | solution.py:82
  791.5 48.2 %psum.15 = f32[]{:T(128)} all-reduce(f32[]{:T(128)} %get-tuple-element.4), channel_id=1, replica_groups=mesh['tok'=16,'blk'=2] {'tok','blk'}, use_global_device_ids=true, to_apply=%region_2.3 | all-reduce | flops 1 | bytes 8 | tf_op jit(solution)/shard_map/psum | solution.py:83
  840.4 1.2 fusion.11
  841.6 5.5 pmax.15
  847.1 6.5 fusion.1
  (9 shorter events, 0.1 us)
Async XLA Ops:
  7.2 651.0 %all-gather.2.cloned.1.call-start = ((), (), s32[]{:S(2)}) async-start(), calls=%async_computation | async-start | bytes 15597568 | tf_op jit(solution)/shard_map/all_gather | solution.py:71
  149.9 326.1 %copy-start.1 = (f32[3584]{0:T(1024)S(1)}, f32[3584]{0:T(1024)}, u32[]{:S(2)}) copy-start(f32[3584]{0:T(1024)} %param.3) | copy-start | bytes 43012
  149.9 326.1 %copy-start = (bf16[128,3584]{1,0:T(8,128)(2,1)S(1)}, bf16[128,3584]{1,0:T(8,128)(2,1)}, u32[]{:S(2)}) copy-start(bf16[128,3584]{1,0:T(8,128)(2,1)} %param.2) | copy-start | bytes 2752516
  500.3 41.9 %collective-permute-start = (f32[128,3584]{1,0:T(8,128)S(1)}, f32[128,3584]{1,0:T(8,128)}, u32[]{:S(2)}, u32[]{:S(2)}) collective-permute-start(f32[128,3584]{1,0:T(8,128)S(1)} %fusion.3), channel_id=1, source_target_pairs={{0,1},{1,0},{2,3},{3,2},{4,5},{5,4},{6,7},{7,6},{8,9},{9,8},{10,11... | collective-permute-start | bytes 5505032 | tf_op jit(solution)/shard_map/ppermute | solution.py:24
  545.0 179.4 %all-reduce.2.cloned.1.call-start = ((), (), s32[]{:S(2)}) async-start(), calls=%async_computation.1 | async-start | bytes 4194304 | tf_op jit(solution)/shard_map/psum | solution.py:29
Sparse Core Ops, SparseCore 0:
  545.1 113.0 all-gather.1
  662.7 61.6 all-reduce.1
where the time goes:
time: 867 us; the launch traced here: 860 us
  local copies, waits for them, and re-layouts  326 us (38%)
  waiting for transfers between devices  216 us (25%)
  other arithmetic  157 us (18%)
  blocking collectives  107 us (12%)
  matrix products  38.4 us (4%)
  between operations  14.8 us (2%)
    mul x1, local copies, waits for them, and re-layouts, per_device(): jnp.kron(walsh_table(local_walsh) / math.sqrt(local_walsh), cosine_table(...  326 us
    mul x1, other arithmetic, per_device(): jnp.kron(walsh_table(local_walsh) / math.sqrt(local_walsh), cosine_table(...  142 us
    all_gather x1, waiting for transfers between devices, per_device(): all_tokens = lax.all_gather(rotated, 'tok', axis=0, tiled=True)  113 us
    psum x1, waiting for transfers between devices, from_root(): return lax.psum(kept, axis)  61.7 us
    pmax x1, blocking collectives, per_device(): column_peak = lax.pmax(local_peaks, 'tok')  53.1 us
    psum x1, blocking collectives, per_device(): lax.psum(jnp.sum(jnp.where(on_diag, gram_block, 0.0)), ('tok', 'blk'))  48.2 us
    ppermute x1, waiting for transfers between devices, swapped(): return lax.ppermute(block, axis, route)  41.4 us
    dot_general x1, matrix products, per_device(): jnp.dot(signed.astype(jnp.float32), local_table, precision=lax.Precision....  24.3 us
  transfers between devices with their start and end apart: 3, of which 3 were waited for; matrix products, arithmetic and copies ran while one was open for 0% of the time, Pallas kernels for 0%

commit v1 on v0

v1 whole, which is shorter than its diff:
```python
import functools
import math

import jax
import jax.numpy as jnp
import numpy as np
from jax import lax
from jax.experimental import pallas as pl
from jax.experimental.pallas import tpu as pltpu
from jax.sharding import PartitionSpec as P

WALSH = 512
MIX = 14
FEATURES = 7168

EPS = 1e-06
DAMP = 0.01

LANES = 128
UNIT_WALSH = LANES // math.gcd(LANES, MIX)
UNIT = UNIT_WALSH * MIX


def parity(number):
    return bin(number).count("1") & 1


def unit_tables():
    walsh = np.array(
        [[1 - 2 * parity(i & j) for j in range(UNIT_WALSH)] for i in range(UNIT_WALSH)], np.float64
    )
    k = np.arange(MIX)[:, None]
    n = np.arange(MIX)[None, :]
    cosine = math.sqrt(2.0 / MIX) * np.cos(math.pi * (n + 0.5) * k / MIX)
    cosine[0] *= math.sqrt(0.5)
    table = np.kron(walsh, cosine.T).astype(np.float32)
    high = table.astype(jnp.bfloat16)
    low = (table - high.astype(np.float32)).astype(jnp.bfloat16)
    return high, low


def rotate_kernel(blocks, chunks, high_ref, low_ref, flips_ref, *refs):
    pieces, (out_ref, square_ref) = refs[:blocks], refs[blocks:]
    mixed = []
    for c in range(chunks):
        total = None
        for k in range(blocks):
            part = pieces[k][:, c * UNIT : (c + 1) * UNIT]
            value = jnp.dot(part, high_ref[...], preferred_element_type=jnp.float32)
            value += jnp.dot(part, low_ref[...], preferred_element_type=jnp.float32)
            value = value * flips_ref[0, k]
            total = value if total is None else total + value
        mixed.append(total)
    step = 1
    while step < chunks:
        for low in range(chunks):
            if not low & step:
                a, b = mixed[low], mixed[low | step]
                mixed[low], mixed[low | step] = a + b, a - b
        step *= 2
    square = jnp.float32(0.0)
    for c in range(chunks):
        rounded = (mixed[c] * (1.0 / math.sqrt(WALSH))).astype(jnp.bfloat16)
        out_ref[:, c * UNIT : (c + 1) * UNIT] = rounded
        wide = rounded.astype(jnp.float32)
        square += jnp.sum(wide * wide)
    square_ref[...] = jnp.full(square_ref.shape, square, jnp.float32)


def rotate(pieces, flips):
    blocks = len(pieces)
    rows, width = pieces[0].shape
    high, low = unit_tables()
    vmem = pl.BlockSpec(memory_space=pltpu.VMEM)
    return pl.pallas_call(
        functools.partial(rotate_kernel, blocks, width // UNIT),
        out_shape=(
            jax.ShapeDtypeStruct((rows, width), jnp.bfloat16),
            jax.ShapeDtypeStruct((8, LANES), jnp.float32),
        ),
        in_specs=[vmem, vmem, pl.BlockSpec(memory_space=pltpu.SMEM)] + [vmem] * blocks,
        out_specs=(vmem, vmem),
        compiler_params=pltpu.CompilerParams(vmem_limit_bytes=48 * 1024 * 1024),
        name="rotate",
    )(jnp.asarray(high), jnp.asarray(low), flips, *pieces)


def gram_kernel(rows, skew_ref, scale_ref, window_ref, columns_ref, hessian_ref, peak_ref, best):
    tile = pl.program_id(0)
    width = columns_ref.shape[1]
    skew = skew_ref[0, 0]
    diagonal = skew_ref[0, 1] - tile * width
    inverse = scale_ref[0, 0]
    block = lax.dot_general(
        window_ref[...], columns_ref[...], (((0,), (0,)), ((), ())), preferred_element_type=jnp.float32
    )
    whole = window_ref.shape[1]
    if whole == rows:
        block = block[:rows]
    else:
        other = whole - rows
        block = jnp.where(skew == 0, block[:rows], block[other:])
    row = lax.broadcasted_iota(jnp.int32, (rows, width), 0) + diagonal
    column = lax.broadcasted_iota(jnp.int32, (rows, width), 1)
    on_diag = row == column
    hessian_ref[...] = block * inverse + jnp.where(on_diag, DAMP, 0.0)
    size = jnp.where(on_diag, 0.0, jnp.abs(block))
    most = size[:, :LANES]
    for j in range(1, width // LANES):
        most = jnp.maximum(most, size[:, j * LANES : (j + 1) * LANES])

    @pl.when(tile == 0)
    def _():
        best[...] = most

    @pl.when(tile > 0)
    def _():
        best[...] = jnp.maximum(best[...], most)

    @pl.when(tile == pl.num_programs(0) - 1)
    def _():
        flat = jnp.max(best[...], axis=1, keepdims=True)
        turned = jnp.transpose(jnp.broadcast_to(flat, (rows, LANES)))
        peak_ref[...] = turned[:8] * inverse


def gram(window, columns, rows, skew, diagonal, inverse):
    tokens, width = columns.shape
    tile = 512 if width % 512 == 0 else LANES
    smem = pl.BlockSpec(memory_space=pltpu.SMEM)
    numbers = jnp.stack([skew, diagonal]).astype(jnp.int32).reshape(1, 2)
    return pl.pallas_call(
        functools.partial(gram_kernel, rows),
        grid=(width // tile,),
        out_shape=(
            jax.ShapeDtypeStruct((rows, width), jnp.float32),
            jax.ShapeDtypeStruct((8, rows), jnp.float32),
        ),
        in_specs=[
            smem,
            smem,
            pl.BlockSpec((tokens, window.shape[1]), lambda i: (0, 0)),
            pl.BlockSpec((tokens, tile), lambda i: (0, i)),
        ],
        out_specs=(
            pl.BlockSpec((rows, tile), lambda i: (0, i)),
            pl.BlockSpec((8, rows), lambda i: (0, 0)),
        ),
        scratch_shapes=[pltpu.VMEM((rows, LANES), jnp.float32)],
        compiler_params=pltpu.CompilerParams(vmem_limit_bytes=48 * 1024 * 1024),
        cost_estimate=pl.CostEstimate(
            flops=2 * rows * width * tokens,
            bytes_accessed=2 * tokens * width + 4 * rows * width,
            transcendentals=0,
        ),
        name="gram",
    )(numbers, inverse.reshape(1, 1), window, columns)


def per_device(activations, signs):
    tok_rows, block_width = activations.shape
    blocks = lax.axis_size("blk")
    me = lax.axis_index("blk")
    token_groups = lax.axis_size("tok")
    token_index = lax.axis_index("tok")
    signed = activations * signs.astype(jnp.bfloat16)[None, :]
    pieces, flips = [], []
    for k in range(blocks):
        piece = signed
        if k:
            piece = lax.ppermute(signed, "blk", [(i, i ^ k) for i in range(blocks)])
        pieces.append(piece)
        table = jnp.asarray([1.0 - 2.0 * parity(i & (i ^ k)) for i in range(blocks)], jnp.float32)
        flips.append(table[me])
    rotated, squares = rotate(pieces, jnp.stack(flips).reshape(1, blocks))
    trace_total = lax.psum(squares[0, 0], ("tok", "blk"))
    diag_mean = trace_total / FEATURES + EPS
    inverse = 1.0 / diag_mean

    row_count = FEATURES // token_groups
    window = -(-row_count // LANES) * LANES
    all_tokens = lax.all_gather(rotated, "tok", axis=0, tiled=True)
    first_row = token_index * row_count
    owner = first_row // block_width
    offset = first_row - owner * block_width
    start = jnp.minimum(offset // LANES * LANES, block_width - window)
    skew = offset - start
    own = lax.dynamic_slice_in_dim(all_tokens, start, window, 1)
    if blocks == 2:
        partner = lax.ppermute(own, "blk", [(0, 1), (1, 0)])
        rows_window = jnp.where(owner == me, own, partner)
    else:
        rows_window = lax.psum(jnp.where(owner == me, own, 0).astype(own.dtype), "blk")
    hessian, peak = gram(
        rows_window, all_tokens, row_count, skew, first_row - me * block_width, inverse
    )
    peaks = lax.all_gather(peak[0], ("blk", "tok"), axis=0).reshape(blocks, FEATURES)
    ratios = jnp.max(peaks, axis=0)
    incoherence = lax.dynamic_slice_in_dim(ratios, me * block_width, block_width, 0)
    return (hessian, incoherence, jnp.max(ratios))


def solution(mesh):
    in_specs = (P("tok", "blk"), P("blk"))
    out_specs = (P("tok", "blk"), P("blk"), P())
    return jax.shard_map(
        per_device, mesh=mesh, in_specs=in_specs, out_specs=out_specs, check_vma=False
    )
```

time: 867 us -> 308 us (0.36)
  local copies, waits for them, and re-layouts: 326 us -> 8.74 us
  other arithmetic: 157 us -> 6.24 us
  waiting for transfers between devices: 216 us -> 133 us
  matrix products: 38.4 us -> 0 us
  Pallas kernels: 0 us -> 21 us
  blocking collectives: 107 us -> 117 us
    mul x1 -> x0, local copies, waits for them, and re-layouts: 326 us -> none  [per_device(): jnp.kron(walsh_table(local_walsh) / math.sqrt(local_walsh), cosine_table(...]
    mul x2 -> x1, other arithmetic: 142 us -> 1.24 us  [per_device(): signed = activations * signs.astype(jnp.bfloat16)[None, :]]
    psum x1 -> x0, waiting for transfers between devices: 61.7 us -> none  [from_root(): return lax.psum(kept, axis)]
    pmax x2 -> x0, blocking collectives: 58.6 us -> none  [the longest x1 53.1 us: per_device(): column_peak = lax.pmax(local_peaks, 'tok')]
    dot_general x2 -> x0, matrix products: 38.4 us -> none  [the longest x1 24.3 us: per_device(): jnp.dot(signed.astype(jnp.float32), local_table, precision=lax.Precision....]
    all_gather x0 -> x1, blocking collectives: none -> 35.9 us  [per_device(): lax.all_gather(peak[0], ('blk', 'tok'), axis=0).reshape(blocks, FEATURES)]
    psum x1, blocking collectives: 48.2 us -> 81.5 us  [per_device(): trace_total = lax.psum(squares[0, 0], ('tok', 'blk'))]
    ppermute x1 -> x2, waiting for transfers between devices: 41.4 us -> 19.7 us  [the longest x1 19.7 us: per_device(): piece = lax.ppermute(signed, 'blk', [(i, i ^ k) for i in range(blocks)])]
  transfers between devices with their start and end apart: 3 -> 3, of which waited for: 3 -> 2; matrix products, arithmetic and copies ran while one was open for 0% -> 1% of each run, Pallas kernels for 0% -> 0%
where the time goes in v1:
time: 308 us; the launch traced here: 302 us
  waiting for transfers between devices  133 us (43%)
  blocking collectives  117 us (38%)
  Pallas kernels  21 us (7%)
  between operations  14.8 us (5%)
  local copies, waits for them, and re-layouts  8.74 us (3%)
  other arithmetic  6.24 us (2%)
    all_gather x1, waiting for transfers between devices, per_device(): all_tokens = lax.all_gather(rotated, 'tok', axis=0, tiled=True)  113 us
    psum x1, blocking collectives, per_device(): trace_total = lax.psum(squares[0, 0], ('tok', 'blk'))  81.5 us
    all_gather x1, blocking collectives, per_device(): lax.all_gather(peak[0], ('blk', 'tok'), axis=0).reshape(blocks, FEATURES)  35.9 us
    ppermute x1, waiting for transfers between devices, per_device(): piece = lax.ppermute(signed, 'blk', [(i, i ^ k) for i in range(blocks)])  19.7 us
    pallas_call x1, Pallas kernels, gram(): pl.pallas_call(functools.partial(gram_kernel, rows), grid=(width // tile,...  14.4 us
    pallas_call x1, Pallas kernels, rotate(): pl.pallas_call(functools.partial(rotate_kernel, blocks, width // UNIT), o...  6.58 us
  transfers between devices with their start and end apart: 3, of which 2 were waited for; matrix products, arithmetic and copies ran while one was open for 1% of the time, Pallas kernels for 0%

profile of v1, /device:TPU:12, one launch (start us, length us, event | category | flops | bytes accessed | tf_op | source)
XLA Modules:
  0.0 302.2 jit_solution(6010465578238480187)
XLA Ops:
  7.2 0.0 copy-start
  7.2 0.0 all-gather.3.cloned.1.call-start
  7.2 0.8 convert_element_type.3
  8.1 1.2 broadcast_multiply_fusion.refs_0_
  9.3 0.6 collective-permute-start
  9.9 1.2 dynamic_slice.12
  11.1 0.6 pad_bitcast_fusion.flips_ref
  11.8 19.7 %collective-permute-done.refs_1_ = bf16[128,3584]{1,0:T(8,128)(2,1)S(1)} collective-permute-done((bf16[128,3584]{1,0:T(8,128)(2,1)S(1)}, bf16[128,3584]{1,0:T(8,128)(2,1)S(1)}, u32[]{:S(2)}, u32[]{:S(2)}) %collective-permute-start) | collective-permute-done | bytes 917536 | tf_op jit(solution)/shard_map/ppermute | solution.py:171
  31.5 0.0 copy-done
  31.5 0.0 copy-start.1
  31.5 1.4 copy-done.1
  32.9 6.6 %rotate.1 = (bf16[128,3584]{1,0:T(8,128)(2,1)}, f32[8,128]{1,0:T(8,128)S(1)}) custom-call(bf16[896,896]{1,0:T(8,128)(2,1)S(1)} %copy-done.1, bf16[896,896]{1,0:T(8,128)(2,1)S(1)} %copy-done, f32[1,2]{1,0:T(1,128)S(1)} %pad_bitcast_fusion.flips_ref, bf16[128,3584]{1,0:T(8,128)(2,1)S(1)} %broadcast_multiply_fusion.refs_0_, ...), custom_call_target="tpu_custom_call" | custom-call | tf_op jit(solution)/shard_map/rotate/pallas_call | solution.py:75
  39.5 0.0 all-gather.3.cloned.1.call-update
  39.5 113.2 %all-gather.3.cloned.1.call-done.columns_ref = bf16[2048,3584]{1,0:T(8,128)(2,1)} async-done(((bf16[128,3584]{1,0:T(8,128)(2,1)}), bf16[2048,3584]{1,0:T(8,128)(2,1)}) %all-gather.3.cloned.1.call-update) | async-done | bytes 14680080 | tf_op jit(solution)/shard_map/all_gather | solution.py:182
  152.7 4.1 %constant_dynamic-slice_fusion = bf16[2048,512]{1,0:T(8,128)(2,1)} fusion(bf16[2048,3584]{1,0:T(8,128)(2,1)} %all-gather.3.cloned.1.call-done.columns_ref, s32[]{:T(128)S(6)} %select_n.30), kind=kLoop, calls=%fused_computation.5 | loop fusion | bytes 4194308 | tf_op jit(solution)/shard_map/dynamic_slice | solution.py:188
  156.8 0.6 collective-permute-start.1
  157.4 0.1 add_bitcast_fusion.skew_ref
  157.4 0.5 slice.6
  158.0 81.5 %psum.7 = f32[]{:T(128)} all-reduce(f32[]{:T(128)} %bitcast.4), channel_id=1, replica_groups=mesh['tok'=16,'blk'=2] {'tok','blk'}, use_global_device_ids=true, to_apply=%region_0.0 | all-reduce | flops 1 | bytes 8 | tf_op jit(solution)/shard_map/psum | solution.py:176
  240.2 0.0 collective-permute-done.1
  240.2 3.2 %broadcast_select_fusion.window_ref = bf16[2048,512]{1,0:T(8,128)(2,1)S(1)} fusion(bf16[2048,512]{1,0:T(8,128)(2,1)S(1)} %collective-permute-done.1, pred[]{:T(512)S(6)} %eq.3, bf16[2048,3584]{1,0:T(8,128)(2,1)} %all-gather.3.cloned.1.call-done.columns_ref, s32[]{:T(128)S(6)} %select_n.30), kind=kLoop, calls=%fused_computation | loop fusion | flops 1048576 | bytes 6291461 | tf_op jit(solution)/shard_map/jit(_where)/select_n | solution.py:191
  243.4 14.4 %gram.1 = (f32[448,3584]{1,0:T(8,128)}, f32[8,448]{1,0:T(8,128)S(1)}) custom-call(s32[1,2]{1,0:T(1,128)S(1)} %add_bitcast_fusion.skew_ref, f32[1,1]{1,0:T(1,128)} %bitcast.5.scale_ref, bf16[2048,512]{1,0:T(8,128)(2,1)S(1)} %broadcast_select_fusion.window_ref, bf16[2048,3584]{1,0:T(8,128)(2,1)} %all-gather.3.cloned.1.call-done.columns_ref), custom_call_target="tpu_custom_call" | custom-call | flops 6576668672 | bytes 21102592 | tf_op jit(solution)/shard_map/gram/pallas_call | solution.py:132
  257.8 35.9 %all-gather = f32[32,1,448]{2,1,0:T(1,128)S(1)} all-gather(f32[1,1,448]{2,1,0:T(1,128)S(1)} %slice_bitcast_fusion), channel_id=1, replica_groups=mesh['tok'=16,'blk'=2] {'blk','tok'}, dimensions={0}, use_global_device_ids=true | all-gather | bytes 59136 | tf_op jit(solution)/shard_map/all_gather | solution.py:197
  293.7 0.8 fusion
  294.5 0.1 reshape.22
  294.6 0.1 reduce_max.18
  294.7 0.7 dynamic_slice.15
  (1 shorter events, 0.0 us)
Async XLA Ops:
  7.2 24.3 %copy-start = (bf16[896,896]{1,0:T(8,128)(2,1)S(1)}, bf16[896,896]{1,0:T(8,128)(2,1)}, u32[]{:S(2)}) copy-start(bf16[896,896]{1,0:T(8,128)(2,1)} %constant.60.clone.low_ref) | copy-start | bytes 4816900
  7.2 145.5 %all-gather.3.cloned.1.call-start = ((), (), s32[]{:S(2)}) async-start(), calls=%async_computation | async-start | bytes 15597568 | tf_op jit(solution)/shard_map/all_gather | solution.py:182
  9.3 22.2 %collective-permute-start = (bf16[128,3584]{1,0:T(8,128)(2,1)S(1)}, bf16[128,3584]{1,0:T(8,128)(2,1)S(1)}, u32[]{:S(2)}, u32[]{:S(2)}) collective-permute-start(bf16[128,3584]{1,0:T(8,128)(2,1)S(1)} %broadcast_multiply_fusion.refs_0_), channel_id=1, source_target_pairs={{0,1},{1,0},{2,3},{3,2},{4,5},{5,4},{6,7},{7,6},{8,9},{9,8},{10,11... | collective-permute-start | bytes 2752520 | tf_op jit(solution)/shard_map/ppermute | solution.py:171
  31.5 1.4 copy-start.1
  156.8 83.4 %collective-permute-start.1 = (bf16[2048,512]{1,0:T(8,128)(2,1)}, bf16[2048,512]{1,0:T(8,128)(2,1)S(1)}, u32[]{:S(2)}, u32[]{:S(2)}) collective-permute-start(bf16[2048,512]{1,0:T(8,128)(2,1)} %constant_dynamic-slice_fusion), channel_id=1, source_target_pairs={{0,1},{1,0},{2,3},{3,2},{4,5},{5,4},{6,7},{7,6},{8,9},{9,8},{10,11... | collective-permute-start | bytes 6291464 | tf_op jit(solution)/shard_map/ppermute | solution.py:190
Sparse Core Ops, SparseCore 0:
  39.6 113.0 all-gather.2

commit v2 on v1

--- a/solution.py
+++ b/solution.py
@@ -19,6 +19,7 @@
 LANES = 128
 UNIT_WALSH = LANES // math.gcd(LANES, MIX)
 UNIT = UNIT_WALSH * MIX
+MESH = pl.DeviceIdType.MESH
 
 
 def parity(number):
@@ -85,21 +86,295 @@
     )(jnp.asarray(high), jnp.asarray(low), flips, *pieces)
 
 
-def gram_kernel(rows, skew_ref, scale_ref, window_ref, columns_ref, hessian_ref, peak_ref, best):
+def place(tok, row_count, width, window):
+    first = tok * row_count
+    owner = first // width
+    offset = first - owner * width
+    start = jnp.minimum(offset // LANES * LANES, width - window)
+    return owner, start, offset - start
+
+
+def greet_all(tok, blk):
+    tokens, blocks = lax.axis_size("tok"), lax.axis_size("blk")
+    count = tokens * blocks
+    barrier = pltpu.get_barrier_semaphore()
+    me = tok * blocks + blk
+
+    @pl.loop(1, count)
+    def _(k):
+        other = lax.rem(me + k, count)
+        pl.semaphore_signal(
+            barrier, inc=1, device_id={"tok": other // blocks, "blk": other % blocks}, device_id_type=MESH
+        )
+
+    pl.semaphore_wait(barrier, count - 1)
+
+
+def broadcast_start(tok, blk, src, dst, send, recv):
+    tokens, blocks = lax.axis_size("tok"), lax.axis_size("blk")
+    count = tokens * blocks
+    me = tok * blocks + blk
+
+    @pl.loop(1, count)
+    def _(k):
+        other = lax.rem(me + k, count)
+        pltpu.make_async_remote_copy(
+            src, dst.at[me], send, recv,
+            device_id={"tok": other // blocks, "blk": other % blocks}, device_id_type=MESH,
+        ).start()
+
+
+def broadcast_wait(tok, blk, dst, send, recv):
+    count = dst.shape[0] - 1
+    both = pltpu.make_async_remote_copy(
+        dst.at[pl.ds(0, count)], dst.at[pl.ds(0, count)], send, recv,
+        device_id={"tok": tok, "blk": blk}, device_id_type=MESH,
+    )
+    both.wait_send()
+    both.wait_recv()
+
+
+def spread_kernel(src, dst, local, send, recv):
+    tok, blk = lax.axis_index("tok"), lax.axis_index("blk")
+    greet_all(tok, blk)
+    broadcast_start(tok, blk, src, dst, send, recv)
+    own = pltpu.make_async_copy(src, dst.at[tok * lax.axis_size("blk") + blk], local)
+    own.start()
+    own.wait()
+    broadcast_wait(tok, blk, dst, send, recv)
+
+
+def spread(block):
+    count = lax.axis_size("tok") * lax.axis_size("blk")
+    vmem = pl.BlockSpec(memory_space=pltpu.VMEM)
+    return pl.pallas_call(
+        spread_kernel,
+        out_shape=jax.ShapeDtypeStruct((count,) + block.shape, block.dtype),
+        in_specs=[vmem],
+        out_specs=vmem,
+        scratch_shapes=[pltpu.SemaphoreType.DMA] * 3,
+        compiler_params=pltpu.CompilerParams(collective_id=1, has_side_effects=True),
+        name="spread",
+    )(block)
+
+
+def gather_kernel(
+    depth, across, sub, early, row_count, rot, part, cols, rows, parts,
+    local, recv, pair_send, pair_recv, z_send, x_send, y_send, y_recv, part_local, part_send, part_recv,
+):
+    tok, blk = lax.axis_index("tok"), lax.axis_index("blk")
+    blocks = lax.axis_size("blk")
+    tok_rows, width = rot.shape
+    window = rows.shape[1]
+    half = cols.shape[0] // 2
+    steps = tok_rows // sub
+    core, chip = tok % 2, tok // 2
+    z, x = chip // across, chip % across
+
+    greet_all(tok, blk)
+    own_rows = pltpu.make_async_copy(rot, cols.at[pl.ds(pl.multiple_of(tok * tok_rows, sub), tok_rows)], local)
+    own_rows.start()
+
+    def first_row(oz, ox, s):
+        return pl.multiple_of(((oz * across + ox) * 2 + core) * tok_rows + s * sub, sub)
+
+    def remote(src, dst, send, arrive, to_tok, to_blk):
+        return pltpu.make_async_remote_copy(
+            src, dst, send, arrive, device_id={"tok": to_tok, "blk": to_blk}, device_id_type=MESH
+        )
+
+    def fan(src, oz, ox, s, z_ways, x_ways):
+        row = first_row(oz, ox, s)
+        dst = cols.at[pl.ds(row, sub)]
+        arrive = recv.at[(oz * across + ox) * steps + s]
+        for way in x_ways:
+
+            @pl.when((x + way >= 0) & (x + way < across))
+            def _():
+                remote(src, dst, x_send.at[(way + 1) // 2], arrive, tok + 2 * way, blk).start()
+
+        for way in z_ways:
+
+            @pl.when((z + way >= 0) & (z + way < depth))
+            def _():
+                remote(src, dst, z_send.at[(way + 1) // 2], arrive, tok + 2 * across * way, blk).start()
+
+        remote(src, dst, pair_send, pair_recv, tok + 1 - 2 * core, blk).start()
+        for j in range(2):
+            owner, start, _ = place(chip * 2 + j, row_count, width, window)
+
+            @pl.when(owner == blk)
+            def _():
+                part_src = src.at[:, pl.ds(pl.multiple_of(start, LANES), window)]
+                for k in range(1, blocks):
+                    remote(
+                        part_src, rows.at[pl.ds(row, sub)], y_send.at[2 * k + j], y_recv,
+                        chip * 2 + j, lax.rem(blk + k, blocks),
+                    ).start()
+
+    def relay(oz, ox, s, z_ways, x_ways):
+        piece = cols.at[pl.ds(first_row(oz, ox, s), sub)]
+        remote(piece, piece, pair_send, recv.at[(oz * across + ox) * steps + s], tok, blk).wait_recv()
+        fan(piece, oz, ox, s, z_ways, x_ways)
+
+    @pl.loop(0, steps)
+    def _(s):
+        fan(rot.at[pl.ds(pl.multiple_of(s * sub, sub), sub)], z, x, s, (1, -1), (1, -1))
+
+    broadcast_start(tok, blk, part, parts, part_send, part_recv)
+    own_part = pltpu.make_async_copy(part, parts.at[tok * blocks + blk], part_local)
+    own_part.start()
+
+    for dx in range(1, across):
+        for way in (1, -1):
+            ox = x - way * dx
+
+            @pl.when((ox >= 0) & (ox < across))
+            def _():
+                for s in range(early):
+                    relay(z, ox, s, (1, -1), (way,))
+
+    for dz in range(1, depth):
+
+        @pl.loop(early, steps)
+        def _(s):
+            for way in (1, -1):
+                oz = z - way * dz
+
+                @pl.when((oz >= 0) & (oz < depth))
+                def _():
+                    relay(oz, x, s, (way,), (1, -1))
+
+        for way in (1, -1):
+            oz = z - way * dz
+
+            @pl.when((oz >= 0) & (oz < depth))
+            def _():
+                @pl.loop(0, across * early)
+                def _(n):
+                    relay(oz, n // early, n % early, (way,), ())
+
+    for dx in range(1, across):
+        for way in (1, -1):
+            ox = x - way * dx
+
+            @pl.when((ox >= 0) & (ox < across))
+            def _():
+                for dz in range(depth):
+                    for side in (1, -1) if dz else (1,):
+                        oz = z - side * dz
+
+                        @pl.when((oz >= 0) & (oz < depth))
+                        def _():
+                            @pl.loop(early, steps)
+                            def _(s):
+                                relay(oz, ox, s, (), (way,))
+
+    def settle(count, send):
+        piece = cols.at[pl.ds(0, count)]
+        remote(piece, piece, send, pair_recv, tok, blk).wait_send()
+
+    late = steps - early
+    for v in range(depth):
+        @pl.when(z == v)
+        def _():
+            unit = (late + early * across) * sub
+            if v < depth - 1:
+                settle((v + 1) * unit, z_send.at[1])
+            if v > 0:
+                settle((depth - v) * unit, z_send.at[0])
+
+    for v in range(across):
+        @pl.when(x == v)
+        def _():
+            unit = (late * depth + early) * sub
+            if v < across - 1:
+                settle((v + 1) * unit, x_send.at[1])
+            if v > 0:
+                settle((across - v) * unit, x_send.at[0])
+
+    settle(half, pair_send)
+    for j in range(2):
+        owner, _, _ = place(chip * 2 + j, row_count, width, window)
+
+        @pl.when(owner == blk)
+        def _():
+            piece = rows.at[pl.ds(0, half)]
+            for k in range(1, blocks):
+                remote(piece, piece, y_send.at[2 * k + j], y_recv, tok, blk).wait_send()
+
+    piece = cols.at[pl.ds(0, half)]
+    remote(piece, piece, pair_send, pair_recv, tok, blk).wait_recv()
+    owner, _, _ = place(tok, row_count, width, window)
+
+    @pl.when(owner != blk)
+    def _():
+        remote(rows, rows, pair_send, y_recv, tok, blk).wait_recv()
+
+    own_rows.wait()
+    own_part.wait()
+    broadcast_wait(tok, blk, parts, part_send, part_recv)
+
+
+def gather(rotated, squares, window, row_count):
+    tok_rows, width = rotated.shape
+    groups, blocks = lax.axis_size("tok"), lax.axis_size("blk")
+    depth = 4 if groups % 8 == 0 else 1
+    across = groups // (2 * depth)
+    sub = 16
+    steps = tok_rows // sub
+    dma = pltpu.SemaphoreType.DMA
+    vmem = pl.BlockSpec(memory_space=pltpu.VMEM)
+    anywhere = pl.BlockSpec(memory_space=pl.ANY)
+    return pl.pallas_call(
+        functools.partial(gather_kernel, depth, across, sub, 1, row_count),
+        out_shape=(
+            jax.ShapeDtypeStruct((groups * tok_rows, width), rotated.dtype),
+            jax.ShapeDtypeStruct((groups * tok_rows, window), rotated.dtype),
+            jax.ShapeDtypeStruct((groups * blocks,) + squares.shape, squares.dtype),
+        ),
+        in_specs=[vmem, vmem],
+        out_specs=(anywhere, anywhere, vmem),
+        scratch_shapes=[
+            dma, dma((groups // 2 * steps,)), dma, dma, dma((2,)), dma((2,)), dma((2 * blocks,)), dma,
+            dma, dma, dma,
+        ],
+        compiler_params=pltpu.CompilerParams(
+            collective_id=0, has_side_effects=True, vmem_limit_bytes=16 * 1024 * 1024
+        ),
+        name="gather",
+    )(rotated, squares)
+
+
+def gram_kernel(rows, scale_ref, window_ref, all_ref, columns_ref, hessian_ref, peak_ref, best, left, sem):
     tile = pl.program_id(0)
     width = columns_ref.shape[1]
-    skew = skew_ref[0, 0]
-    diagonal = skew_ref[0, 1] - tile * width
+    tok, blk = lax.axis_index("tok"), lax.axis_index("blk")
+    whole = window_ref.shape[1]
+    block_width = all_ref.shape[1]
+    owner, start, skew = place(tok, rows, block_width, whole)
+    diagonal = tok * rows - blk * block_width - tile * width
     inverse = scale_ref[0, 0]
+
+    @pl.when((tile == 0) & (owner == blk))
+    def _():
+        own = pltpu.make_async_copy(all_ref.at[:, pl.ds(pl.multiple_of(start, LANES), whole)], left, sem)
+        own.start()
+        own.wait()
+
+    @pl.when((tile == 0) & (owner != blk))
+    def _():
+        given = pltpu.make_async_copy(window_ref, left, sem)
+        given.start()
+        given.wait()
+
     block = lax.dot_general(
-        window_ref[...], columns_ref[...], (((0,), (0,)), ((), ())), preferred_element_type=jnp.float32
+        left[...], columns_ref[...], (((0,), (0,)), ((), ())), preferred_element_type=jnp.float32
     )
-    whole = window_ref.shape[1]
     if whole == rows:
         block = block[:rows]
     else:
-        other = whole - rows
-        block = jnp.where(skew == 0, block[:rows], block[other:])
+        block = jnp.where(skew == 0, block[:rows], block[whole - rows :])
     row = lax.broadcasted_iota(jnp.int32, (rows, width), 0) + diagonal
     column = lax.broadcasted_iota(jnp.int32, (rows, width), 1)
     on_diag = row == column
@@ -124,11 +399,10 @@
         peak_ref[...] = turned[:8] * inverse
 
 
-def gram(window, columns, rows, skew, diagonal, inverse):
+def gram(window, columns, rows, inverse):
     tokens, width = columns.shape
     tile = 512 if width % 512 == 0 else LANES
-    smem = pl.BlockSpec(memory_space=pltpu.SMEM)
-    numbers = jnp.stack([skew, diagonal]).astype(jnp.int32).reshape(1, 2)
+    anywhere = pl.BlockSpec(memory_space=pl.ANY)
     return pl.pallas_call(
         functools.partial(gram_kernel, rows),
         grid=(width // tile,),
@@ -137,16 +411,20 @@
             jax.ShapeDtypeStruct((8, rows), jnp.float32),
         ),
         in_specs=[
-            smem,
-            smem,
-            pl.BlockSpec((tokens, window.shape[1]), lambda i: (0, 0)),
+            pl.BlockSpec(memory_space=pltpu.SMEM),
+            anywhere,
+            anywhere,
             pl.BlockSpec((tokens, tile), lambda i: (0, i)),
         ],
         out_specs=(
             pl.BlockSpec((rows, tile), lambda i: (0, i)),
             pl.BlockSpec((8, rows), lambda i: (0, 0)),
         ),
-        scratch_shapes=[pltpu.VMEM((rows, LANES), jnp.float32)],
+        scratch_shapes=[
+            pltpu.VMEM((rows, LANES), jnp.float32),
+            pltpu.VMEM(window.shape, window.dtype),
+            pltpu.SemaphoreType.DMA,
+        ],
         compiler_params=pltpu.CompilerParams(vmem_limit_bytes=48 * 1024 * 1024),
         cost_estimate=pl.CostEstimate(
             flops=2 * rows * width * tokens,
@@ -154,7 +432,7 @@
             transcendentals=0,
         ),
         name="gram",
-    )(numbers, inverse.reshape(1, 1), window, columns)
+    )(inverse.reshape(1, 1), window, columns, columns)
 
 
 def per_device(activations, signs):
@@ -162,7 +440,6 @@
     blocks = lax.axis_size("blk")
     me = lax.axis_index("blk")
     token_groups = lax.axis_size("tok")
-    token_index = lax.axis_index("tok")
     signed = activations * signs.astype(jnp.bfloat16)[None, :]
     pieces, flips = [], []
     for k in range(blocks):
@@ -173,29 +450,14 @@
         table = jnp.asarray([1.0 - 2.0 * parity(i & (i ^ k)) for i in range(blocks)], jnp.float32)
         flips.append(table[me])
     rotated, squares = rotate(pieces, jnp.stack(flips).reshape(1, blocks))
-    trace_total = lax.psum(squares[0, 0], ("tok", "blk"))
-    diag_mean = trace_total / FEATURES + EPS
-    inverse = 1.0 / diag_mean
-
     row_count = FEATURES // token_groups
     window = -(-row_count // LANES) * LANES
-    all_tokens = lax.all_gather(rotated, "tok", axis=0, tiled=True)
-    first_row = token_index * row_count
-    owner = first_row // block_width
-    offset = first_row - owner * block_width
-    start = jnp.minimum(offset // LANES * LANES, block_width - window)
-    skew = offset - start
-    own = lax.dynamic_slice_in_dim(all_tokens, start, window, 1)
-    if blocks == 2:
-        partner = lax.ppermute(own, "blk", [(0, 1), (1, 0)])
-        rows_window = jnp.where(owner == me, own, partner)
-    else:
-        rows_window = lax.psum(jnp.where(owner == me, own, 0).astype(own.dtype), "blk")
-    hessian, peak = gram(
-        rows_window, all_tokens, row_count, skew, first_row - me * block_width, inverse
-    )
-    peaks = lax.all_gather(peak[0], ("blk", "tok"), axis=0).reshape(blocks, FEATURES)
-    ratios = jnp.max(peaks, axis=0)
+    all_tokens, rows_window, parts = gather(rotated, squares, window, row_count)
+    trace_total = jnp.sum(parts[:, 0, 0])
+    diag_mean = trace_total / FEATURES + EPS
+    hessian, peak = gram(rows_window, all_tokens, row_count, 1.0 / diag_mean)
+    peaks = spread(peak)[:, 0, :]
+    ratios = jnp.max(peaks.reshape(token_groups, blocks, row_count), axis=1).reshape(FEATURES)
     incoherence = lax.dynamic_slice_in_dim(ratios, me * block_width, block_width, 0)
     return (hessian, incoherence, jnp.max(ratios))
 

time: 308 us -> 172 us (0.56); the launches traced: 302 us -> 170 us
  blocking collectives: 117 us -> 0 us
  waiting for transfers between devices: 133 us -> 19.7 us
  Pallas kernels: 21 us -> 134 us
  between operations: 14.8 us -> 1.41 us
    pallas_call x0 -> x2, Pallas kernels: none -> 114 us  [the longest x1 82.3 us: gather(): pl.pallas_call(functools.partial(gather_kernel, depth, across, sub, 1, ro...]
    all_gather x1 -> x0, waiting for transfers between devices: 113 us -> none  [per_device(): all_tokens = lax.all_gather(rotated, 'tok', axis=0, tiled=True)]
    psum x1 -> x0, blocking collectives: 81.5 us -> none  [per_device(): trace_total = lax.psum(squares[0, 0], ('tok', 'blk'))]
    all_gather x1 -> x0, blocking collectives: 35.9 us -> none  [per_device(): lax.all_gather(peak[0], ('blk', 'tok'), axis=0).reshape(blocks, FEATURES)]
    unnamed x5 -> x8, local copies, waits for them, and re-layouts: 1.43 us -> 7.23 us
    dynamic_slice x1 -> x0, local copies, waits for them, and re-layouts: 4.12 us -> none  [per_device(): own = lax.dynamic_slice_in_dim(all_tokens, start, window, 1)]
    select_n x1 -> x0, other arithmetic: 3.22 us -> none  [per_device(): rows_window = jnp.where(owner == me, own, partner)]
  transfers between devices with their start and end apart: 3 -> 1, of which waited for: 2 -> 1; matrix products, arithmetic and copies ran while one was open for 1% -> 1% of each run, Pallas kernels for 0% -> 0%
where the time goes in v2:
time: 172 us; the launch traced here: 170 us
  Pallas kernels  134 us (78%)
  waiting for transfers between devices  19.7 us (11%)
  local copies, waits for them, and re-layouts  9.92 us (6%)
  other arithmetic  4.64 us (3%)
    pallas_call x1, Pallas kernels, gather(): pl.pallas_call(functools.partial(gather_kernel, depth, across, sub, 1, ro...  82.3 us
    pallas_call x1, Pallas kernels, spread(): pl.pallas_call(spread_kernel, out_shape=jax.ShapeDtypeStruct((count,) + b...  31.5 us
    ppermute x1, waiting for transfers between devices, per_device(): piece = lax.ppermute(signed, 'blk', [(i, i ^ k) for i in range(blocks)])  19.7 us
    pallas_call x1, Pallas kernels, gram(): pl.pallas_call(functools.partial(gram_kernel, rows), grid=(width // tile,...  14.5 us
    unnamed x8, local copies, waits for them, and re-layouts  7.23 us
    pallas_call x1, Pallas kernels, rotate(): pl.pallas_call(functools.partial(rotate_kernel, blocks, width // UNIT), o...  5.62 us
  transfers between devices with their start and end apart: 1, of which 1 were waited for; matrix products, arithmetic and copies ran while one was open for 1% of the time, Pallas kernels for 0%

profile of v2, /device:TPU:12, one launch (start us, length us, event | category | flops | bytes accessed | tf_op | source)
XLA Modules:
  0.0 170.2 jit_solution(7797106632443361147)
XLA Ops:
  0.6 0.0 copy-start.1
  0.6 0.8 convert_element_type.3
  1.5 1.2 broadcast_multiply_fusion.refs_0_
  2.7 0.6 collective-permute-start
  3.3 1.2 dynamic_slice.9
  4.5 0.6 pad_bitcast_fusion.flips_ref
  5.2 19.7 %collective-permute-done.refs_1_ = bf16[128,3584]{1,0:T(8,128)(2,1)S(1)} collective-permute-done((bf16[128,3584]{1,0:T(8,128)(2,1)S(1)}, bf16[128,3584]{1,0:T(8,128)(2,1)S(1)}, u32[]{:S(2)}, u32[]{:S(2)}) %collective-permute-start) | collective-permute-done | bytes 917536 | tf_op jit(solution)/shard_map/ppermute | solution.py:448
  24.9 0.0 copy-done.1
  24.9 0.0 copy-start.2
  24.9 1.4 copy-done.2
  26.3 5.6 %rotate.1 = (bf16[128,3584]{1,0:T(8,128)(2,1)S(1)}, f32[8,128]{1,0:T(8,128)S(1)}) custom-call(bf16[896,896]{1,0:T(8,128)(2,1)S(1)} %copy-done.2, bf16[896,896]{1,0:T(8,128)(2,1)S(1)} %copy-done.1, f32[1,2]{1,0:T(1,128)S(1)} %pad_bitcast_fusion.flips_ref, bf16[128,3584]{1,0:T(8,128)(2,1)S(1)} %broadcast_multiply_fusion.refs_0_, ...), custom_call_target="tpu_custom_call" | custom-call | tf_op jit(solution)/shard_map/rotate/pallas_call | solution.py:76
  31.9 82.3 %gather.1 = (bf16[2048,3584]{1,0:T(8,128)(2,1)S(1)}, bf16[2048,512]{1,0:T(8,128)(2,1)S(1)}, f32[32,8,128]{2,1,0:T(8,128)S(1)}) custom-call(bf16[128,3584]{1,0:T(8,128)(2,1)S(1)} %get-tuple-element.10.rot, f32[8,128]{1,0:T(8,128)S(1)} %get-tuple-element.11.part), custom_call_target="tpu_custom_call" | custom-call | tf_op jit(solution)/shard_map/gather/pallas_call | solution.py:329
  114.3 0.0 copy-start
  114.3 5.2 %copy-done = bf16[2048,3584]{1,0:T(8,128)(2,1)} copy-done((bf16[2048,3584]{1,0:T(8,128)(2,1)}, bf16[2048,3584]{1,0:T(8,128)(2,1)S(1)}, u32[]{:S(2)}) %copy-start) | copy-done | bytes 14680088
  119.5 0.6 slice_reduce_fusion.2
  120.8 14.5 %gram.1 = (f32[448,3584]{1,0:T(8,128)}, f32[8,448]{1,0:T(8,128)S(1)}) custom-call(f32[1,1]{1,0:T(1,128)} %bitcast.1.scale_ref, bf16[2048,512]{1,0:T(8,128)(2,1)S(1)} %get-tuple-element.13.window_ref, bf16[2048,3584]{1,0:T(8,128)(2,1)} %copy-done, bf16[2048,3584]{1,0:T(8,128)(2,1)} %copy-done), custom_call_target="tpu_custom_call" | custom-call | flops 6576668672 | bytes 21102592 | tf_op jit(solution)/shard_map/gram/pallas_call | solution.py:406
  135.3 0.0 copy-start.3
  135.4 0.6 copy-done.3
  136.0 31.5 %spread.1 = f32[32,8,448]{2,1,0:T(8,128)} custom-call(f32[8,448]{1,0:T(8,128)} %copy-done.3), custom_call_target="tpu_custom_call" | custom-call | tf_op jit(solution)/shard_map/spread/pallas_call | solution.py:150
  167.5 1.8 %slice_reduce_fusion = (f32[]{:T(128)}, f32[32,448]{1,0:T(8,128)S(1)}) fusion(f32[32,8,448]{2,1,0:T(8,128)} %spread.1), kind=kLoop, calls=%fused_computation.1 | loop fusion | flops 14335 | bytes 114692 | tf_op jit(solution)/shard_map/reduce_max | solution.py:462
  169.4 0.1 reduce_max.18
  169.5 0.1 reshape.18
  169.6 0.7 dynamic_slice.11
  (1 shorter events, 0.0 us)
Async XLA Ops:
  0.6 24.3 %copy-start.1 = (bf16[896,896]{1,0:T(8,128)(2,1)S(1)}, bf16[896,896]{1,0:T(8,128)(2,1)}, u32[]{:S(2)}) copy-start(bf16[896,896]{1,0:T(8,128)(2,1)} %constant.34.clone.low_ref) | copy-start | bytes 4816900
  2.7 22.2 %collective-permute-start = (bf16[128,3584]{1,0:T(8,128)(2,1)S(1)}, bf16[128,3584]{1,0:T(8,128)(2,1)S(1)}, u32[]{:S(2)}, u32[]{:S(2)}) collective-permute-start(bf16[128,3584]{1,0:T(8,128)(2,1)S(1)} %broadcast_multiply_fusion.refs_0_), channel_id=1, source_target_pairs={{0,1},{1,0},{2,3},{3,2},{4,5},{5,4},{6,7},{7,6},{8,9},{9,8},{10,11... | collective-permute-start | bytes 2752520 | tf_op jit(solution)/shard_map/ppermute | solution.py:448
  24.9 1.4 copy-start.2
  114.3 5.2 %copy-start = (bf16[2048,3584]{1,0:T(8,128)(2,1)}, bf16[2048,3584]{1,0:T(8,128)(2,1)S(1)}, u32[]{:S(2)}) copy-start(bf16[2048,3584]{1,0:T(8,128)(2,1)S(1)} %get-tuple-element.14.all_ref.columns_ref) | copy-start | bytes 44040196
  135.3 0.6 copy-start.3

commit v3 on v2

--- a/solution.py
+++ b/solution.py
@@ -346,7 +346,7 @@
     )(rotated, squares)
 
 
-def gram_kernel(rows, scale_ref, window_ref, all_ref, columns_ref, hessian_ref, peak_ref, best, left, sem):
+def gram_kernel(rows, scale_ref, window_ref, all_ref, columns_ref, hessian_ref, peak_ref, best, left, turned_left, sem):
     tile = pl.program_id(0)
     width = columns_ref.shape[1]
     tok, blk = lax.axis_index("tok"), lax.axis_index("blk")
@@ -368,9 +368,11 @@
         given.start()
         given.wait()
 
-    block = lax.dot_general(
-        left[...], columns_ref[...], (((0,), (0,)), ((), ())), preferred_element_type=jnp.float32
-    )
+    @pl.when(tile == 0)
+    def _():
+        turned_left[...] = jnp.transpose(left[...])
+
+    block = jnp.dot(turned_left[...], columns_ref[...], preferred_element_type=jnp.float32)
     if whole == rows:
         block = block[:rows]
     else:
@@ -423,9 +425,10 @@
         scratch_shapes=[
             pltpu.VMEM((rows, LANES), jnp.float32),
             pltpu.VMEM(window.shape, window.dtype),
+            pltpu.VMEM(window.shape[::-1], window.dtype),
             pltpu.SemaphoreType.DMA,
         ],
-        compiler_params=pltpu.CompilerParams(vmem_limit_bytes=48 * 1024 * 1024),
+        compiler_params=pltpu.CompilerParams(vmem_limit_bytes=60 * 1024 * 1024),
         cost_estimate=pl.CostEstimate(
             flops=2 * rows * width * tokens,
             bytes_accessed=2 * tokens * width + 4 * rows * width,

time: 172 us -> 175 us (1.017)
  Pallas kernels: 134 us -> 136 us
    pallas_call x1, Pallas kernels: 14.5 us -> 16.7 us  [gram(): pl.pallas_call(functools.partial(gram_kernel, rows), grid=(width // tile,...]
where the time goes in v3:
time: 175 us; the launch traced here: 173 us
  Pallas kernels  136 us (78%)
  waiting for transfers between devices  19.7 us (11%)
  local copies, waits for them, and re-layouts  10.7 us (6%)
  other arithmetic  4.64 us (3%)
    pallas_call x1, Pallas kernels, gather(): pl.pallas_call(functools.partial(gather_kernel, depth, across, sub, 1, ro...  82.3 us
    pallas_call x1, Pallas kernels, spread(): pl.pallas_call(spread_kernel, out_shape=jax.ShapeDtypeStruct((count,) + b...  31.6 us
    ppermute x1, waiting for transfers between devices, per_device(): piece = lax.ppermute(signed, 'blk', [(i, i ^ k) for i in range(blocks)])  19.7 us
    pallas_call x1, Pallas kernels, gram(): pl.pallas_call(functools.partial(gram_kernel, rows), grid=(width // tile,...  16.7 us
    unnamed x8, local copies, waits for them, and re-layouts  7.97 us
    pallas_call x1, Pallas kernels, rotate(): pl.pallas_call(functools.partial(rotate_kernel, blocks, width // UNIT), o...  5.62 us
  transfers between devices with their start and end apart: 1, of which 1 were waited for; matrix products, arithmetic and copies ran while one was open for 1% of the time, Pallas kernels for 0%

profile of v3, /device:TPU:12, one launch (start us, length us, event | category | flops | bytes accessed | tf_op | source)
XLA Modules:
  0.0 173.1 jit_solution(1236763759669589112)
XLA Ops:
  0.6 0.0 copy-start.2
  0.6 0.8 convert_element_type.3
  1.5 1.2 broadcast_multiply_fusion.refs_0_
  2.7 0.6 collective-permute-start
  3.3 1.2 dynamic_slice.9
  4.5 0.6 pad_bitcast_fusion.flips_ref
  5.2 19.7 %collective-permute-done.refs_1_ = bf16[128,3584]{1,0:T(8,128)(2,1)S(1)} collective-permute-done((bf16[128,3584]{1,0:T(8,128)(2,1)S(1)}, bf16[128,3584]{1,0:T(8,128)(2,1)S(1)}, u32[]{:S(2)}, u32[]{:S(2)}) %collective-permute-start) | collective-permute-done | bytes 917536 | tf_op jit(solution)/shard_map/ppermute | solution.py:451
  24.9 0.0 copy-done.2
  24.9 0.0 copy-start.3
  24.9 1.4 copy-done.3
  26.3 5.6 %rotate.1 = (bf16[128,3584]{1,0:T(8,128)(2,1)S(1)}, f32[8,128]{1,0:T(8,128)S(1)}) custom-call(bf16[896,896]{1,0:T(8,128)(2,1)S(1)} %copy-done.3, bf16[896,896]{1,0:T(8,128)(2,1)S(1)} %copy-done.2, f32[1,2]{1,0:T(1,128)S(1)} %pad_bitcast_fusion.flips_ref, bf16[128,3584]{1,0:T(8,128)(2,1)S(1)} %broadcast_multiply_fusion.refs_0_, ...), custom_call_target="tpu_custom_call" | custom-call | tf_op jit(solution)/shard_map/rotate/pallas_call | solution.py:76
  31.9 82.3 %gather.1 = (bf16[2048,3584]{1,0:T(8,128)(2,1)S(1)}, bf16[2048,512]{1,0:T(8,128)(2,1)S(1)}, f32[32,8,128]{2,1,0:T(8,128)S(1)}) custom-call(bf16[128,3584]{1,0:T(8,128)(2,1)S(1)} %get-tuple-element.10.rot, f32[8,128]{1,0:T(8,128)S(1)} %get-tuple-element.11.part), custom_call_target="tpu_custom_call" | custom-call | tf_op jit(solution)/shard_map/gather/pallas_call | solution.py:329
  114.3 0.0 copy-start
  114.3 5.2 %copy-done = bf16[2048,3584]{1,0:T(8,128)(2,1)} copy-done((bf16[2048,3584]{1,0:T(8,128)(2,1)}, bf16[2048,3584]{1,0:T(8,128)(2,1)S(1)}, u32[]{:S(2)}) %copy-start) | copy-done | bytes 14680088
  119.5 0.0 copy-start.1
  119.5 1.3 copy-done.1
  120.8 0.6 slice_reduce_fusion.2
  122.1 16.7 %gram.1 = (f32[448,3584]{1,0:T(8,128)}, f32[8,448]{1,0:T(8,128)}) custom-call(f32[1,1]{1,0:T(1,128)} %bitcast.1.scale_ref, bf16[2048,512]{1,0:T(8,128)(2,1)} %copy-done.1, bf16[2048,3584]{1,0:T(8,128)(2,1)} %copy-done, bf16[2048,3584]{1,0:T(8,128)(2,1)} %copy-done), custom_call_target="tpu_custom_call" | custom-call | flops 6576668672 | bytes 21102592 | tf_op jit(solution)/shard_map/gram/pallas_call | solution.py:408
  138.8 31.6 %spread.1 = f32[32,8,448]{2,1,0:T(8,128)} custom-call(f32[8,448]{1,0:T(8,128)} %get-tuple-element.16.src), custom_call_target="tpu_custom_call" | custom-call | tf_op jit(solution)/shard_map/spread/pallas_call | solution.py:150
  170.4 1.8 %slice_reduce_fusion = (f32[]{:T(128)}, f32[32,448]{1,0:T(8,128)S(1)}) fusion(f32[32,8,448]{2,1,0:T(8,128)} %spread.1), kind=kLoop, calls=%fused_computation.1 | loop fusion | flops 14335 | bytes 114692 | tf_op jit(solution)/shard_map/reduce_max | solution.py:465
  172.3 0.1 reduce_max.18
  172.4 0.1 reshape.18
  172.5 0.7 dynamic_slice.11
  (1 shorter events, 0.0 us)
Async XLA Ops:
  0.6 24.3 %copy-start.2 = (bf16[896,896]{1,0:T(8,128)(2,1)S(1)}, bf16[896,896]{1,0:T(8,128)(2,1)}, u32[]{:S(2)}) copy-start(bf16[896,896]{1,0:T(8,128)(2,1)} %constant.34.clone.low_ref) | copy-start | bytes 4816900
  2.7 22.2 %collective-permute-start = (bf16[128,3584]{1,0:T(8,128)(2,1)S(1)}, bf16[128,3584]{1,0:T(8,128)(2,1)S(1)}, u32[]{:S(2)}, u32[]{:S(2)}) collective-permute-start(bf16[128,3584]{1,0:T(8,128)(2,1)S(1)} %broadcast_multiply_fusion.refs_0_), channel_id=1, source_target_pairs={{0,1},{1,0},{2,3},{3,2},{4,5},{5,4},{6,7},{7,6},{8,9},{9,8},{10,11... | collective-permute-start | bytes 2752520 | tf_op jit(solution)/shard_map/ppermute | solution.py:451
  24.9 1.4 copy-start.3
  114.3 5.2 %copy-start = (bf16[2048,3584]{1,0:T(8,128)(2,1)}, bf16[2048,3584]{1,0:T(8,128)(2,1)S(1)}, u32[]{:S(2)}) copy-start(bf16[2048,3584]{1,0:T(8,128)(2,1)S(1)} %get-tuple-element.14.all_ref.columns_ref) | copy-start | bytes 44040196
  119.5 1.3 copy-start.1
